TPU v7x, 256 devices: a whole 4x4x8 slice. The times are simulated.
256 devices in a mesh: rep: 8 (over x_lo, y), tp: 8 (over z), fs: 4 (over x_hi, core).
Axes of the slice: x: 4 (x_hi: 2, x_lo: 2; x = x_hi * 2 + x_lo), y: 4, z: 8, core: 2. Of those that a mesh axis runs over, the one named last changes fastest.
Arguments:
- hidden: bfloat16 [64, 8192], P(('rep', 'fs'), 'tp'), may hold values from -6 to 6
- cache_key: bfloat16 [64, 2048, 1024], P(('rep', 'fs'), None, 'tp'), may hold values from -1300 to 1300
- cache_value: bfloat16 [64, 2048, 1024], P(('rep', 'fs'), None, 'tp'), may hold values from -6 to 6
- lengths: int32 [64], P(('rep', 'fs')), may hold values from 8 to 2047
- owner: int32 [1], replicated, may hold values from 0 to 32767
- query_weight: bfloat16 [8, 8192, 4096], P('rep', 'fs', 'tp'), may hold values from -0.0625 to 0.0625
- key_weight: bfloat16 [8, 8192, 1024], P('rep', 'fs', 'tp'), may hold values from -0.0625 to 0.0625
- value_weight: bfloat16 [8, 8192, 1024], P('rep', 'fs', 'tp'), may hold values from -0.0625 to 0.0625
- out_weight: bfloat16 [8, 4096, 8192], P('rep', 'tp', 'fs'), may hold values from -0.09375 to 0.09375
Outputs:
- mixed: bfloat16 [64, 8192], P(('rep', 'fs'), 'tp')
- new_key: bfloat16 [64, 1024], P(('rep', 'fs'), 'tp')
- new_value: bfloat16 [64, 1024], P(('rep', 'fs'), 'tp')
- fresh_query: bfloat16 [8, 8192, 4096], P('rep', 'fs', 'tp')
- fresh_key: bfloat16 [8, 8192, 1024], P('rep', 'fs', 'tp')
- fresh_value: bfloat16 [8, 8192, 1024], P('rep', 'fs', 'tp')
- fresh_out: bfloat16 [8, 4096, 8192], P('rep', 'tp', 'fs')
Inputs may be any that keep to these rules, and one draw needn't show every extreme that they name: `lengths`: the number of positions already in each sequence's cache; the new token stands at that position.
All inputs are finite; a program needn't handle non-finite values.
Results may differ from a plain program's by a relative error of at most 0.0065.
Values may be sent and summed in bfloat16 or wider, within the bound.
No kernel may reach another device: no remote copies, remote signals or barrier semaphores. Data moves between devices by JAX's collectives and lax.ppermute only.
A program may use at most 64 MiB of HBM per device.

v0:
```python
import jax
import jax.numpy as jnp
from jax import lax
from jax.sharding import PartitionSpec as P

DH = 128
rope_base = 500000.0
epsilon = 1e-05


def from_root(shard, axis, root):
    mine = lax.axis_index(axis) == root
    return lax.psum(jnp.where(mine, shard, jnp.zeros_like(shard)), axis)


def cut_along(shard, dim, peers):
    lengths = shard.shape
    parts = shard.reshape(*lengths[:dim], peers, lengths[dim] // peers, *lengths[dim + 1 :])
    return jnp.moveaxis(parts, dim, 0)


def sent_and_summed(shard, axis, dim):
    peers = lax.axis_size(axis)
    parts = lax.all_to_all(cut_along(shard, dim, peers), axis, 0, 0, tiled=True)
    return jnp.sum(parts, axis=0)


def copy_for_each(shard, axis):
    peers = lax.axis_size(axis)
    return lax.all_to_all(
        jnp.broadcast_to(shard[None], (peers, *shard.shape)), axis, 0, 0, tiled=True
    )


def joined_along(parts, dim):
    parts = jnp.moveaxis(parts, 0, dim)
    lengths = parts.shape
    return parts.reshape(*lengths[:dim], lengths[dim] * lengths[dim + 1], *lengths[dim + 2 :])


def collect(shard, axis, dim):
    parts = copy_for_each(shard, axis)
    return joined_along(parts, dim)


def rotate(heads, positions):
    half_dim = heads.shape[-1] // 2
    frequency = rope_base ** (-(jnp.arange(half_dim, dtype=jnp.float32) * 2.0 / heads.shape[-1]))
    angles = positions.astype(jnp.float32)[:, None] * frequency[None, :]
    cosine = jnp.cos(angles)[:, None, :]
    sine_part = jnp.sin(angles)[:, None, :]
    first_half = heads[..., :half_dim]
    second_half = heads[..., half_dim:]
    return jnp.concatenate(
        [
            first_half * cosine - second_half * sine_part,
            second_half * cosine + first_half * sine_part,
        ],
        axis=-1,
    )


def attend(query, own_key, own_value, cache_key, cache_value, lengths):
    seqs, span, width = cache_key.shape
    kv_local = query.shape[1]
    head_size = query.shape[3]
    keys_view = cache_key.reshape(seqs, span, kv_local, head_size)
    values_view = cache_value.reshape(seqs, span, kv_local, head_size)
    scale = head_size ** (-0.5)
    scores = (
        jnp.einsum("shgd,sthd->shgt", query, keys_view, preferred_element_type=jnp.float32) * scale
    )
    own_score = (
        jnp.einsum("shgd,shd->shg", query, own_key, preferred_element_type=jnp.float32) * scale
    )
    live = (jnp.arange(span, dtype=jnp.int32)[None, :] < lengths[:, None])[:, None, None, :]
    masked = jnp.where(live, scores, -jnp.inf)
    row_max = jnp.maximum(jnp.max(masked, axis=-1), own_score)
    weights = jnp.where(live, jnp.exp(scores - row_max[..., None]), 0.0)
    own_weight = jnp.exp(own_score - row_max)
    denominator = jnp.sum(weights, axis=-1) + own_weight
    probs = (weights / denominator[..., None]).astype(jnp.bfloat16)
    own_prob = (own_weight / denominator).astype(jnp.bfloat16)
    context = jnp.einsum("shgt,sthd->shgd", probs, values_view, preferred_element_type=jnp.float32)
    return (
        context
        + own_prob.astype(jnp.float32)[..., None] * own_value.astype(jnp.float32)[:, :, None, :]
    )


def local(
    hidden,
    cache_key,
    cache_value,
    lengths,
    owner,
    query_weight,
    key_weight,
    value_weight,
    out_weight,
):
    owner_rank = owner[0] % lax.axis_size("rep")
    features = lax.all_gather(hidden, "tp", axis=1, tiled=True)
    hidden_wide = features.astype(jnp.float32)
    normed = (
        hidden_wide
        * lax.rsqrt(jnp.mean(hidden_wide * hidden_wide, axis=-1, keepdims=True) + epsilon)
    ).astype(jnp.bfloat16)
    fresh_query, fresh_key, fresh_value, fresh_out = (
        from_root(query_weight, "rep", owner_rank),
        from_root(key_weight, "rep", owner_rank),
        from_root(value_weight, "rep", owner_rank),
        from_root(out_weight, "rep", owner_rank),
    )
    query_rows = fresh_query[0]
    key_rows = fresh_key[0]
    value_rows = fresh_value[0]
    out_cols = fresh_out[0]
    seqs = normed.shape[0]
    query_width = query_rows.shape[1]
    key_width = key_rows.shape[1]
    token_block = lax.all_to_all(normed, "fs", split_axis=1, concat_axis=0, tiled=True)
    joined = sent_and_summed(
        jnp.concatenate(
            [
                jnp.dot(token_block, query_rows, preferred_element_type=jnp.float32),
                jnp.dot(token_block, key_rows, preferred_element_type=jnp.float32),
                jnp.dot(token_block, value_rows, preferred_element_type=jnp.float32),
            ],
            axis=1,
        ),
        "fs",
        0,
    )
    query_proj = joined[:, :query_width]
    key_proj = joined[:, query_width : query_width + key_width]
    value_proj = joined[:, query_width + key_width :]
    q_heads = query_proj.shape[1] // DH
    kv_heads = key_proj.shape[1] // DH
    query_rot = rotate(query_proj.reshape(seqs, q_heads, DH), lengths).astype(jnp.bfloat16)
    query_rot = query_rot.reshape(seqs, kv_heads, q_heads // kv_heads, DH)
    key_new = rotate(key_proj.reshape(seqs, kv_heads, DH), lengths).astype(jnp.bfloat16)
    value_new = value_proj.astype(jnp.bfloat16).reshape(seqs, kv_heads, DH)
    context = attend(query_rot, key_new, value_new, cache_key, cache_value, lengths)
    context = context.astype(jnp.bfloat16).reshape(seqs, q_heads * DH)
    group_context = collect(context, "fs", 0)
    partial_out = jnp.dot(group_context, out_cols, preferred_element_type=jnp.float32)
    terms = lax.all_to_all(partial_out, "fs", split_axis=0, concat_axis=1, tiled=True)
    summed = sent_and_summed(terms, "tp", 1)
    mixed = (summed + hidden.astype(jnp.float32)).astype(jnp.bfloat16)
    return (
        mixed,
        key_new.reshape(seqs, kv_heads * DH),
        value_new.reshape(seqs, kv_heads * DH),
        fresh_query,
        fresh_key,
        fresh_value,
        fresh_out,
    )


def solution(mesh):
    return jax.shard_map(
        local,
        mesh=mesh,
        in_specs=(
            P(("rep", "fs"), "tp"),
            P(("rep", "fs"), None, "tp"),
            P(("rep", "fs"), None, "tp"),
            P(("rep", "fs")),
            P(),
            P("rep", "fs", "tp"),
            P("rep", "fs", "tp"),
            P("rep", "fs", "tp"),
            P("rep", "tp", "fs"),
        ),
        out_specs=(
            P(("rep", "fs"), "tp"),
            P(("rep", "fs"), "tp"),
            P(("rep", "fs"), "tp"),
            P("rep", "fs", "tp"),
            P("rep", "fs", "tp"),
            P("rep", "fs", "tp"),
            P("rep", "tp", "fs"),
        ),
        check_vma=False,
    )
```

profile of v0, /device:TPU:1, one launch (start us, length us, event | category | flops | bytes accessed | tf_op | source)
XLA Modules:
  0.0 207.0 jit_solution(11398649867773513769)
XLA Ops:
  7.2 0.0 copy-start
  7.2 0.0 all-reduce.3.cloned.1.call-start
  8.0 0.0 copy-start.2
  8.0 1.5 broadcast_select_fusion
  9.5 0.9 copy-done.2
  10.3 1.5 broadcast_select_fusion.1
  11.8 0.0 copy-done.7
  11.8 0.1 copy-done.8
  11.9 1.0 broadcast_select_fusion.2
  12.9 0.0 all-reduce.3.cloned.1.call-update
  13.0 0.7 copy-done.9
  13.6 23.1 %all_gather.3 = bf16[2,8192]{1,0:T(2,128)(2,1)S(1)} all-gather(bf16[2,1024]{1,0:T(2,128)(2,1)S(1)} %copy-done.9), channel_id=1, replica_groups=mesh['rep'=8,'tp'=8,'fs'=4] {'tp'}, dimensions={1}, use_global_device_ids=true | all-gather | bytes 36864 | tf_op jit(solution)/shard_map/all_gather | solution.py:103
  36.8 0.2 fusion.10
  36.9 0.7 fusion.11
  37.6 10.9 %all-to-all-start = ((bf16[2,4,2048]{2,0,1:T(2,128)(2,1)}), bf16[2,4,2048]{2,0,1:T(2,128)(2,1)S(1)}, u32[]{:S(2)}, u32[]{:S(2)}) async-start(bf16[2,4,2048]{2,0,1:T(2,128)(2,1)} %bitcast), calls=%async_computation | async-start | bytes 65536 | tf_op jit(solution)/shard_map/all_to_all | solution.py:122
  48.6 0.0 copy-done.10
  48.6 0.1 iota_compare_fusion
  48.7 5.2 %all-to-all-done = bf16[2,4,2048]{2,0,1:T(2,128)(2,1)S(1)} async-done(((bf16[2,4,2048]{2,0,1:T(2,128)(2,1)}), bf16[2,4,2048]{2,0,1:T(2,128)(2,1)S(1)}, u32[]{:S(2)}, u32[]{:S(2)}) %all-to-all-start) | async-done | bytes 32800 | tf_op jit(solution)/shard_map/all_to_all | solution.py:122
  53.9 93.1 %all-reduce.3.cloned.1.call-done = (bf16[1,2048,128]{2,1,0:T(8,128)(2,1)}, bf16[1,2048,128]{2,1,0:T(8,128)(2,1)}, bf16[1,2048,512]{2,1,0:T(8,128)(2,1)}, bf16[1,512,2048]{2,1,0:T(8,128)(2,1)}) async-done(((bf16[1,2048,128]{2,1,0:T(8,128)(2,1)}, bf16[1,2048,128]{2,1,0:T(8,128)(2,1)}, bf16[1,2048,512]{2,1,0:T(8,128)(2,1)}, bf16[1,512,2048]{2,1,0:T(8,128)(2,1)}), (bf16[1,2048,128]{2,1,0:T(8,128)(2,1)}, ...) | async-done | bytes 5242896 | tf_op jit(solution)/shard_map/psum | solution.py:13
  147.0 2.0 fusion.2
  149.1 0.0 copy-done.5
  149.1 0.2 fusion.8
  149.3 0.0 copy-done.3
  149.3 0.2 fusion.6
  149.5 0.6 reshape.245
  150.1 4.8 %all-to-all-start.1 = ((f32[4,2,768]{2,1,0:T(2,128)}), f32[4,2,768]{2,1,0:T(2,128)S(1)}, u32[]{:S(2)}, u32[]{:S(2)}) async-start(f32[4,2,768]{2,1,0:T(2,128)} %reshape.245), calls=%async_computation.1 | async-start | bytes 49152 | tf_op jit(solution)/shard_map/all_to_all | solution.py:24
  154.9 0.1 multiply_cosine_fusion.1
  155.0 4.5 %all-to-all-done.1 = f32[4,2,768]{2,1,0:T(2,128)S(1)} async-done(((f32[4,2,768]{2,1,0:T(2,128)}), f32[4,2,768]{2,1,0:T(2,128)S(1)}, u32[]{:S(2)}, u32[]{:S(2)}) %all-to-all-start.1) | async-done | bytes 24608 | tf_op jit(solution)/shard_map/all_to_all | solution.py:24
  159.6 0.5 fusion.32
  160.1 0.1 fusion.28
  160.2 0.1 fusion.39
  160.3 0.1 subtract_convert_fusion
  160.4 0.2 fusion.25
  160.6 0.0 copy-done
  160.6 0.5 select_reduce_fusion
  161.1 0.2 fusion.12
  161.3 1.5 fusion.5
  162.9 7.7 %all_to_all.47 = bf16[4,2,512]{2,1,0:T(2,128)(2,1)S(1)} all-to-all(bf16[4,2,512]{2,1,0:T(2,128)(2,1)S(1)} %broadcast_in_dim.52), channel_id=1, replica_groups=mesh['rep'=8,'tp'=8,'fs'=4] {'fs'}, dimensions={0} | all-to-all | bytes 16384 | tf_op jit(solution)/shard_map/all_to_all | solution.py:30
  170.6 0.4 fusion
  171.0 8.5 %all_to_all.48 = f32[4,2,2048]{2,1,0:T(2,128)} all-to-all(f32[4,2,2048]{2,1,0:T(2,128)S(1)} %fusion), channel_id=1, replica_groups=mesh['rep'=8,'tp'=8,'fs'=4] {'fs'}, dimensions={0} | all-to-all | bytes 131072 | tf_op jit(solution)/shard_map/all_to_all | solution.py:148
  179.5 6.7 %all-to-all-start.4 = ((f32[8,2,1024]{2,1,0:T(2,128)}), f32[8,2,1024]{2,1,0:T(2,128)S(1)}, u32[]{:S(2)}, u32[]{:S(2)}) async-start(f32[8,2,1024]{2,1,0:T(2,128)} %bitcast.16), calls=%async_computation.4 | async-start | bytes 131072 | tf_op jit(solution)/shard_map/all_to_all | solution.py:24
  186.2 0.6 pad_maximum_fusion.2
  186.8 6.6 %all-to-all-done.4 = f32[8,2,1024]{2,1,0:T(2,128)S(1)} async-done(((f32[8,2,1024]{2,1,0:T(2,128)}), f32[8,2,1024]{2,1,0:T(2,128)S(1)}, u32[]{:S(2)}, u32[]{:S(2)}) %all-to-all-start.4) | async-done | bytes 65568 | tf_op jit(solution)/shard_map/all_to_all | solution.py:24
  193.5 0.6 add_convert_fusion
  194.1 3.1 %copy.34 = bf16[1,2048,512]{2,1,0:T(8,128)(2,1)} copy(bf16[1,2048,512]{2,1,0:T(8,128)(2,1)} %get-tuple-element.28) | data formatting | bytes 4194304
  197.2 0.8 copy.35
  198.0 0.8 copy.36
  198.8 1.3 copy.37
  (26 shorter events, 0.2 us)
Async XLA Ops:
  7.2 153.4 %copy-start = (bf16[2,2048,128]{2,1,0:T(8,128)(2,1)S(1)}, bf16[2,2048,128]{2,1,0:T(8,128)(2,1)}, u32[]{:S(2)}) copy-start(bf16[2,2048,128]{2,1,0:T(8,128)(2,1)} %param.10) | copy-start | bytes 3145732
  7.2 139.8 %all-reduce.3.cloned.1.call-start = ((), (), s32[]{:S(2)}) async-start(), calls=%async_computation.5 | async-start | bytes 10485760 | tf_op jit(solution)/shard_map/psum | solution.py:13
  8.0 2.3 %copy-start.2 = (bf16[1,2048,512]{2,1,0:T(8,128)(2,1)S(1)}, bf16[1,2048,512]{2,1,0:T(8,128)(2,1)}, u32[]{:S(2)}) copy-start(bf16[1,2048,512]{2,1,0:T(8,128)(2,1)} %param.14) | copy-start | bytes 6291460
  10.3 1.5 copy-start.7
  10.3 1.6 copy-start.8
  12.9 0.7 copy-start.9
  12.9 35.6 %copy-start.10 = (s32[2]{0:T(128)S(1)}, s32[2]{0:T(128)}, u32[]{:S(2)}) copy-start(s32[2]{0:T(128)} %param.12) | copy-start | bytes 28
  37.6 16.2 %all-to-all-start = ((bf16[2,4,2048]{2,0,1:T(2,128)(2,1)}), bf16[2,4,2048]{2,0,1:T(2,128)(2,1)S(1)}, u32[]{:S(2)}, u32[]{:S(2)}) async-start(bf16[2,4,2048]{2,0,1:T(2,128)(2,1)} %bitcast), calls=%async_computation | async-start | bytes 65536 | tf_op jit(solution)/shard_map/all_to_all | solution.py:122
  147.0 2.1 copy-start.5
  147.0 2.2 %copy-start.3 = (bf16[1,2048,128]{2,1,0:T(8,128)(2,1)S(1)}, bf16[1,2048,128]{2,1,0:T(8,128)(2,1)}, u32[]{:S(2)}) copy-start(bf16[1,2048,128]{2,1,0:T(8,128)(2,1)} %get-tuple-element.30) | copy-start | bytes 1572868
  149.1 21.5 %copy-start.1 = (bf16[1,512,2048]{2,1,0:T(8,128)(2,1)S(1)}, bf16[1,512,2048]{2,1,0:T(8,128)(2,1)}, u32[]{:S(2)}) copy-start(bf16[1,512,2048]{2,1,0:T(8,128)(2,1)} %get-tuple-element.31) | copy-start | bytes 6291460
  150.1 9.4 %all-to-all-start.1 = ((f32[4,2,768]{2,1,0:T(2,128)}), f32[4,2,768]{2,1,0:T(2,128)S(1)}, u32[]{:S(2)}, u32[]{:S(2)}) async-start(f32[4,2,768]{2,1,0:T(2,128)} %reshape.245), calls=%async_computation.1 | async-start | bytes 49152 | tf_op jit(solution)/shard_map/all_to_all | solution.py:24
  179.5 14.0 %all-to-all-start.4 = ((f32[8,2,1024]{2,1,0:T(2,128)}), f32[8,2,1024]{2,1,0:T(2,128)S(1)}, u32[]{:S(2)}, u32[]{:S(2)}) async-start(f32[8,2,1024]{2,1,0:T(2,128)} %bitcast.16), calls=%async_computation.4 | async-start | bytes 131072 | tf_op jit(solution)/shard_map/all_to_all | solution.py:24
  194.1 3.1 %copy-start.6 = (bf16[1,2048,128]{2,1,0:T(8,128)(2,1)S(1)}, bf16[1,2048,128]{2,1,0:T(8,128)(2,1)}, u32[]{:S(2)}) copy-start(bf16[1,2048,128]{2,1,0:T(8,128)(2,1)} %get-tuple-element.29) | copy-start | bytes 1572868
  194.1 3.9 %copy-start.4 = (bf16[1,2048,128]{2,1,0:T(8,128)(2,1)S(1)}, bf16[1,2048,128]{2,1,0:T(8,128)(2,1)}, u32[]{:S(2)}) copy-start(bf16[1,2048,128]{2,1,0:T(8,128)(2,1)} %get-tuple-element.30) | copy-start | bytes 1572868
Sparse Core Ops, SparseCore 0:
  13.1 133.8 all-reduce.2
where the time goes:
time: 208 us; the launch traced here: 207 us
  waiting for transfers between devices  110 us (53%)
  blocking collectives  39.3 us (19%)
  starting transfers between devices  22.5 us (11%)
  between operations  14.9 us (7%)
  local copies, waits for them, and re-layouts  8.42 us (4%)
  other arithmetic  7.29 us (4%)
  matrix products  5.08 us (2%)
    psum x1, waiting for transfers between devices, from_root(): return lax.psum(jnp.where(mine, shard, jnp.zeros_like(shard)), axis)  93.1 us
    all_gather x1, blocking collectives, local(): features = lax.all_gather(hidden, 'tp', axis=1, tiled=True)  23.1 us
    all_to_all x2, starting transfers between devices, sent_and_summed(): parts = lax.all_to_all(cut_along(shard, dim, peers), axis, 0, 0, tiled=True)  11.5 us
    all_to_all x2, waiting for transfers between devices, sent_and_summed(): parts = lax.all_to_all(cut_along(shard, dim, peers), axis, 0, 0, tiled=True)  11.2 us
    all_to_all x1, starting transfers between devices, local(): lax.all_to_all(normed, 'fs', split_axis=1, concat_axis=0, tiled=True)  10.9 us
    all_to_all x1, blocking collectives, local(): lax.all_to_all(partial_out, 'fs', split_axis=0, concat_axis=1, tiled=True)  8.51 us
    unnamed x27, local copies, waits for them, and re-layouts  7.73 us
    all_to_all x1, blocking collectives, copy_for_each(): lax.all_to_all(jnp.broadcast_to(shard[None], (peers, *shard.shape)), axis...  7.7 us
  transfers between devices with their start and end apart: 4, of which 4 were waited for; matrix products, arithmetic and copies ran while one was open for 1% of the time, Pallas kernels for 0%

commit v1 on v0

--- a/solution.py
+++ b/solution.py
@@ -6,6 +6,11 @@
 DH = 128
 rope_base = 500000.0
 epsilon = 1e-05
+
+
+def gather_from_all(shard, axis, dim):
+    copies = jnp.concatenate([shard] * lax.axis_size(axis), axis=dim)
+    return lax.all_to_all(copies, axis, dim, dim, tiled=True)
 
 
 def from_root(shard, axis, root):
@@ -100,7 +105,7 @@
     out_weight,
 ):
     owner_rank = owner[0] % lax.axis_size("rep")
-    features = lax.all_gather(hidden, "tp", axis=1, tiled=True)
+    features = gather_from_all(hidden, "tp", 1)
     hidden_wide = features.astype(jnp.float32)
     normed = (
         hidden_wide

time: 208 us -> 208 us (level)
  blocking collectives: 39.3 us -> 16.2 us
  waiting for transfers between devices: 110 us -> 123 us
  local copies, waits for them, and re-layouts: 8.42 us -> 13.8 us
  starting transfers between devices: 22.5 us -> 27 us
    all_gather x1 -> x0, blocking collectives: 23.1 us -> none  [local(): features = lax.all_gather(hidden, 'tp', axis=1, tiled=True)]
    all_to_all x0 -> x1, starting transfers between devices: none -> 9 us  [gather_from_all(): return lax.all_to_all(copies, axis, dim, dim, tiled=True)]
    psum x1, waiting for transfers between devices: 93.1 us -> 100 us  [from_root(): return lax.psum(jnp.where(mine, shard, jnp.zeros_like(shard)), axis)]
    all_to_all x0 -> x1, waiting for transfers between devices: none -> 6.79 us  [gather_from_all(): return lax.all_to_all(copies, axis, dim, dim, tiled=True)]
    all_to_all x1, starting transfers between devices: 10.9 us -> 6.39 us  [local(): lax.all_to_all(normed, 'fs', split_axis=1, concat_axis=0, tiled=True)]
    unnamed x27 -> x34, local copies, waits for them, and re-layouts: 7.73 us -> 11.9 us
  transfers between devices with their start and end apart: 4 -> 5, of which waited for: 4 -> 5; matrix products, arithmetic and copies ran while one was open for 1% -> 3% of each run, Pallas kernels for 0% -> 0%
where the time goes in v1:
time: 208 us; the launch traced here: 207 us
  waiting for transfers between devices  123 us (59%)
  starting transfers between devices  27 us (13%)
  blocking collectives  16.2 us (8%)
  between operations  14.9 us (7%)
  local copies, waits for them, and re-layouts  13.8 us (7%)
  other arithmetic  6.61 us (3%)
  matrix products  5.08 us (2%)
    psum x1, waiting for transfers between devices, from_root(): return lax.psum(jnp.where(mine, shard, jnp.zeros_like(shard)), axis)  100 us
    unnamed x34, local copies, waits for them, and re-layouts  11.9 us
    all_to_all x2, starting transfers between devices, sent_and_summed(): parts = lax.all_to_all(cut_along(shard, dim, peers), axis, 0, 0, tiled=True)  11.5 us
    all_to_all x2, waiting for transfers between devices, sent_and_summed(): parts = lax.all_to_all(cut_along(shard, dim, peers), axis, 0, 0, tiled=True)  11.2 us
    all_to_all x1, starting transfers between devices, gather_from_all(): return lax.all_to_all(copies, axis, dim, dim, tiled=True)  9 us
    all_to_all x1, blocking collectives, local(): lax.all_to_all(partial_out, 'fs', split_axis=0, concat_axis=1, tiled=True)  8.52 us
    all_to_all x1, blocking collectives, copy_for_each(): lax.all_to_all(jnp.broadcast_to(shard[None], (peers, *shard.shape)), axis...  7.7 us
    all_to_all x1, waiting for transfers between devices, gather_from_all(): return lax.all_to_all(copies, axis, dim, dim, tiled=True)  6.79 us
  transfers between devices with their start and end apart: 5, of which 5 were waited for; matrix products, arithmetic and copies ran while one was open for 3% of the time, Pallas kernels for 0%

profile of v1, /device:TPU:1, one launch (start us, length us, event | category | flops | bytes accessed | tf_op | source)
XLA Modules:
  0.0 207.0 jit_solution(6164412384185820031)
XLA Ops:
  8.0 1.5 broadcast_select_fusion
  9.5 0.9 copy-done.2
  10.3 1.5 broadcast_select_fusion.1
  11.8 0.1 copy-done.8
  11.9 1.0 broadcast_select_fusion.2
  13.0 0.7 copy-done.9
  13.6 0.6 constant_dynamic-update-slice_fusion.7
  14.2 0.6 constant_dynamic-update-slice_fusion.6
  14.8 0.6 constant_dynamic-update-slice_fusion.5
  15.4 0.6 constant_dynamic-update-slice_fusion.4
  16.0 0.6 constant_dynamic-update-slice_fusion.3
  16.6 0.6 constant_dynamic-update-slice_fusion.2
  17.2 0.6 constant_dynamic-update-slice_fusion.1
  17.8 0.6 constant_dynamic-update-slice_fusion
  18.4 9.0 %all-to-all-start = ((bf16[2,8,1024]{2,0,1:T(2,128)(2,1)}), bf16[2,8,1024]{2,0,1:T(2,128)(2,1)S(1)}, u32[]{:S(2)}, u32[]{:S(2)}) async-start(bf16[2,8,1024]{2,0,1:T(2,128)(2,1)} %bitcast), calls=%async_computation | async-start | bytes 65536 | tf_op jit(solution)/shard_map/all_to_all | solution.py:13
  27.4 0.1 iota_compare_fusion
  27.5 6.8 %all-to-all-done = bf16[2,8,1024]{2,0,1:T(2,128)(2,1)S(1)} async-done(((bf16[2,8,1024]{2,0,1:T(2,128)(2,1)}), bf16[2,8,1024]{2,0,1:T(2,128)(2,1)S(1)}, u32[]{:S(2)}, u32[]{:S(2)}) %all-to-all-start) | async-done | bytes 32800 | tf_op jit(solution)/shard_map/all_to_all | solution.py:13
  34.3 0.1 multiply_reduce_fusion
  34.4 0.1 multiply_convert_fusion
  34.5 0.6 copy.22
  35.2 6.4 %all-to-all-start.1 = ((bf16[2,4,2048]{2,0,1:T(2,128)(2,1)}), bf16[2,4,2048]{2,0,1:T(2,128)(2,1)S(1)}, u32[]{:S(2)}, u32[]{:S(2)}) async-start(bf16[2,4,2048]{2,0,1:T(2,128)(2,1)} %copy.22), calls=%async_computation.1 | async-start | bytes 65536 | tf_op jit(solution)/shard_map/all_to_all | solution.py:127
  41.6 5.3 %all-to-all-done.1 = bf16[2,4,2048]{2,0,1:T(2,128)(2,1)S(1)} async-done(((bf16[2,4,2048]{2,0,1:T(2,128)(2,1)}), bf16[2,4,2048]{2,0,1:T(2,128)(2,1)S(1)}, u32[]{:S(2)}, u32[]{:S(2)}) %all-to-all-start.1) | async-done | bytes 32800 | tf_op jit(solution)/shard_map/all_to_all | solution.py:127
  46.8 100.2 %all-reduce.3.cloned.1.call-done = (bf16[1,2048,128]{2,1,0:T(8,128)(2,1)}, bf16[1,2048,128]{2,1,0:T(8,128)(2,1)}, bf16[1,2048,512]{2,1,0:T(8,128)(2,1)}, bf16[1,512,2048]{2,1,0:T(8,128)(2,1)}) async-done(((bf16[1,2048,128]{2,1,0:T(8,128)(2,1)}, bf16[1,2048,128]{2,1,0:T(8,128)(2,1)}, bf16[1,2048,512]{2,1,0:T(8,128)(2,1)}, bf16[1,512,2048]{2,1,0:T(8,128)(2,1)}), (bf16[1,2048,128]{2,1,0:T(8,128)(2,1)}, ...) | async-done | bytes 5242896 | tf_op jit(solution)/shard_map/psum | solution.py:18
  147.0 2.0 fusion.2
  149.1 0.2 fusion.8
  149.3 0.2 fusion.6
  149.5 0.6 reshape.255
  150.1 4.8 %all-to-all-start.2 = ((f32[4,2,768]{2,1,0:T(2,128)}), f32[4,2,768]{2,1,0:T(2,128)S(1)}, u32[]{:S(2)}, u32[]{:S(2)}) async-start(f32[4,2,768]{2,1,0:T(2,128)} %reshape.255), calls=%async_computation.2 | async-start | bytes 49152 | tf_op jit(solution)/shard_map/all_to_all | solution.py:29
  154.9 0.1 multiply_cosine_fusion.1
  155.0 4.5 %all-to-all-done.2 = f32[4,2,768]{2,1,0:T(2,128)S(1)} async-done(((f32[4,2,768]{2,1,0:T(2,128)}), f32[4,2,768]{2,1,0:T(2,128)S(1)}, u32[]{:S(2)}, u32[]{:S(2)}) %all-to-all-start.2) | async-done | bytes 24608 | tf_op jit(solution)/shard_map/all_to_all | solution.py:29
  159.6 0.5 fusion.30
  160.1 0.1 fusion.26
  160.2 0.1 fusion.37
  160.4 0.2 fusion.23
  160.6 0.5 select_reduce_fusion
  161.1 0.2 fusion.10
  161.3 1.5 fusion.5
  162.9 7.7 %all_to_all.53 = bf16[4,2,512]{2,1,0:T(2,128)(2,1)S(1)} all-to-all(bf16[4,2,512]{2,1,0:T(2,128)(2,1)S(1)} %broadcast_in_dim.52), channel_id=1, replica_groups=mesh['rep'=8,'tp'=8,'fs'=4] {'fs'}, dimensions={0} | all-to-all | bytes 16384 | tf_op jit(solution)/shard_map/all_to_all | solution.py:35
  170.6 0.4 fusion
  171.0 8.5 %all_to_all.54 = f32[4,2,2048]{2,1,0:T(2,128)} all-to-all(f32[4,2,2048]{2,1,0:T(2,128)S(1)} %fusion), channel_id=1, replica_groups=mesh['rep'=8,'tp'=8,'fs'=4] {'fs'}, dimensions={0} | all-to-all | bytes 131072 | tf_op jit(solution)/shard_map/all_to_all | solution.py:153
  179.5 6.7 %all-to-all-start.5 = ((f32[8,2,1024]{2,1,0:T(2,128)}), f32[8,2,1024]{2,1,0:T(2,128)S(1)}, u32[]{:S(2)}, u32[]{:S(2)}) async-start(f32[8,2,1024]{2,1,0:T(2,128)} %bitcast.16), calls=%async_computation.5 | async-start | bytes 131072 | tf_op jit(solution)/shard_map/all_to_all | solution.py:29
  186.2 0.6 pad_maximum_fusion.2
  186.8 6.6 %all-to-all-done.5 = f32[8,2,1024]{2,1,0:T(2,128)S(1)} async-done(((f32[8,2,1024]{2,1,0:T(2,128)}), f32[8,2,1024]{2,1,0:T(2,128)S(1)}, u32[]{:S(2)}, u32[]{:S(2)}) %all-to-all-start.5) | async-done | bytes 65568 | tf_op jit(solution)/shard_map/all_to_all | solution.py:29
  193.5 0.6 add_convert_fusion
  194.1 3.1 %copy.49 = bf16[1,2048,512]{2,1,0:T(8,128)(2,1)} copy(bf16[1,2048,512]{2,1,0:T(8,128)(2,1)} %get-tuple-element.28) | data formatting | bytes 4194304
  197.2 0.8 copy.50
  198.0 0.8 copy.51
  198.8 1.3 copy.52
  (38 shorter events, 0.4 us)
Async XLA Ops:
  7.2 153.4 %copy-start = (bf16[2,2048,128]{2,1,0:T(8,128)(2,1)S(1)}, bf16[2,2048,128]{2,1,0:T(8,128)(2,1)}, u32[]{:S(2)}) copy-start(bf16[2,2048,128]{2,1,0:T(8,128)(2,1)} %param.10) | copy-start | bytes 3145732
  7.2 139.8 %all-reduce.3.cloned.1.call-start = ((), (), s32[]{:S(2)}) async-start(), calls=%async_computation.6 | async-start | bytes 10485760 | tf_op jit(solution)/shard_map/psum | solution.py:18
  8.0 2.3 %copy-start.2 = (bf16[1,2048,512]{2,1,0:T(8,128)(2,1)S(1)}, bf16[1,2048,512]{2,1,0:T(8,128)(2,1)}, u32[]{:S(2)}) copy-start(bf16[1,2048,512]{2,1,0:T(8,128)(2,1)} %param.14) | copy-start | bytes 6291460
  10.3 1.5 copy-start.7
  10.3 1.6 copy-start.8
  12.9 0.7 copy-start.9
  12.9 14.4 %copy-start.10 = (s32[2]{0:T(128)S(1)}, s32[2]{0:T(128)}, u32[]{:S(2)}) copy-start(s32[2]{0:T(128)} %param.12) | copy-start | bytes 28
  18.4 15.9 %all-to-all-start = ((bf16[2,8,1024]{2,0,1:T(2,128)(2,1)}), bf16[2,8,1024]{2,0,1:T(2,128)(2,1)S(1)}, u32[]{:S(2)}, u32[]{:S(2)}) async-start(bf16[2,8,1024]{2,0,1:T(2,128)(2,1)} %bitcast), calls=%async_computation | async-start | bytes 65536 | tf_op jit(solution)/shard_map/all_to_all | solution.py:13
  35.2 11.7 %all-to-all-start.1 = ((bf16[2,4,2048]{2,0,1:T(2,128)(2,1)}), bf16[2,4,2048]{2,0,1:T(2,128)(2,1)S(1)}, u32[]{:S(2)}, u32[]{:S(2)}) async-start(bf16[2,4,2048]{2,0,1:T(2,128)(2,1)} %copy.22), calls=%async_computation.1 | async-start | bytes 65536 | tf_op jit(solution)/shard_map/all_to_all | solution.py:127
  147.0 2.1 copy-start.5
  147.0 2.2 %copy-start.3 = (bf16[1,2048,128]{2,1,0:T(8,128)(2,1)S(1)}, bf16[1,2048,128]{2,1,0:T(8,128)(2,1)}, u32[]{:S(2)}) copy-start(bf16[1,2048,128]{2,1,0:T(8,128)(2,1)} %get-tuple-element.30) | copy-start | bytes 1572868
  149.1 21.5 %copy-start.1 = (bf16[1,512,2048]{2,1,0:T(8,128)(2,1)S(1)}, bf16[1,512,2048]{2,1,0:T(8,128)(2,1)}, u32[]{:S(2)}) copy-start(bf16[1,512,2048]{2,1,0:T(8,128)(2,1)} %get-tuple-element.31) | copy-start | bytes 6291460
  150.1 9.4 %all-to-all-start.2 = ((f32[4,2,768]{2,1,0:T(2,128)}), f32[4,2,768]{2,1,0:T(2,128)S(1)}, u32[]{:S(2)}, u32[]{:S(2)}) async-start(f32[4,2,768]{2,1,0:T(2,128)} %reshape.255), calls=%async_computation.2 | async-start | bytes 49152 | tf_op jit(solution)/shard_map/all_to_all | solution.py:29
  179.5 14.0 %all-to-all-start.5 = ((f32[8,2,1024]{2,1,0:T(2,128)}), f32[8,2,1024]{2,1,0:T(2,128)S(1)}, u32[]{:S(2)}, u32[]{:S(2)}) async-start(f32[8,2,1024]{2,1,0:T(2,128)} %bitcast.16), calls=%async_computation.5 | async-start | bytes 131072 | tf_op jit(solution)/shard_map/all_to_all | solution.py:29
  194.1 3.1 %copy-start.6 = (bf16[1,2048,128]{2,1,0:T(8,128)(2,1)S(1)}, bf16[1,2048,128]{2,1,0:T(8,128)(2,1)}, u32[]{:S(2)}) copy-start(bf16[1,2048,128]{2,1,0:T(8,128)(2,1)} %get-tuple-element.29) | copy-start | bytes 1572868
  194.1 3.9 %copy-start.4 = (bf16[1,2048,128]{2,1,0:T(8,128)(2,1)S(1)}, bf16[1,2048,128]{2,1,0:T(8,128)(2,1)}, u32[]{:S(2)}) copy-start(bf16[1,2048,128]{2,1,0:T(8,128)(2,1)} %get-tuple-element.30) | copy-start | bytes 1572868
Sparse Core Ops, SparseCore 0:
  13.1 133.8 all-reduce.2
